TPU v7x, 256 devices: a whole 4x4x8 slice. The times are simulated.
256 devices in a mesh: dp: 128 (over z_hi, x, y, core), tensor: 2 (over z_lo).
Axes of the slice: x: 4, y: 4, z: 8 (z_hi: 4, z_lo: 2; z = z_hi * 2 + z_lo), core: 2. Of those that a mesh axis runs over, the one named last changes fastest.
Arguments:
- tokens: bfloat16 [16384, 1792], P('dp'), may hold values from -6 to 6
- targets: bfloat16 [16384, 1792], P('dp'), may hold values from -6 to 6
- live_mask: int32 [16384], P('dp'), may hold values from 0 to 1, as said below
- up_weight: bfloat16 [1792, 7168], P('dp', 'tensor'), may hold values from -0.125 to 0.125
- down_weight: bfloat16 [1792, 7168], P('dp', 'tensor'), may hold values from -0.0625 to 0.0625
- probe_rows: int32 [1792], replicated, may hold values from 0 to 16777215
- probe_cols: int32 [7168], P('tensor'), may hold values from 0 to 16777215
- moment: float32 [1792, 512], P('dp', 'tensor'), may hold values from 0.01 to 1
Outputs:
- hess_diag: float32 [1792, 512], P('dp', 'tensor')
- second_moment: float32 [1792, 512], P('dp', 'tensor')
- mean_loss: float32 [], replicated
Inputs may be any that keep to these rules, and one draw needn't show every extreme that they name: In every aligned block of 128 tokens the first token has live_mask 1.
All inputs are finite; a program needn't handle non-finite values.
Results may differ from a plain program's by a relative error of at most 0.0023.
Values may be sent and summed in bfloat16 or wider, within the bound.
No kernel may reach another device: no remote copies, remote signals or barrier semaphores. Data moves between devices by JAX's collectives and lax.ppermute only.
A program may use at most 128 MiB of HBM per device.

v0:
```python
import jax
import jax.numpy as jnp
from jax import lax
from jax.sharding import Mesh
from jax.sharding import PartitionSpec as P

BLOCK = 14
DP = ("dp_0", "dp_1", "dp_2", "dp_3")
DP_TENSOR = ("dp_0", "dp_1", "dp_2", "dp_3", "tensor")
gelu_coef = 0.7978845608028654
cubic_coef = 0.044715
beta_two = 0.999


def sent_to_all(shard, axis):
    copies = jnp.broadcast_to(shard, (lax.axis_size(axis), *shard.shape))
    return lax.all_to_all(copies, axis, split_axis=0, concat_axis=0, tiled=True)


def over_copies(shard, axis):
    everything = sent_to_all(shard, axis)
    return jnp.sum(everything, axis=0)


def together(arrays, axis):
    line, at, done = (jnp.concatenate([a.reshape(-1) for a in arrays]), 0, [])
    total = over_copies(line, axis)
    for a in arrays:
        done.append(total[at : at + a.size].reshape(a.shape))
        at += a.size
    return tuple(done)


def cut_along(shard, dim, count):
    before, after = (shard.shape[:dim], shard.shape[dim + 1 :])
    return jnp.moveaxis(shard.reshape(*before, count, -1, *after), dim, 0)


def sent_and_summed(shard, axis, dim):
    count = lax.axis_size(axis)
    tiles = lax.all_to_all(cut_along(shard, dim, count), axis, 0, 0, tiled=True)
    return jnp.sum(tiles, axis=0)


def sum_in_two_steps(shard, axes, dim):
    far, near = axes
    own = sent_and_summed(cut_along(shard, dim, lax.axis_size(far)), near, dim + 1)
    return jnp.sum(lax.all_to_all(own, far, 0, 0, tiled=True), axis=0)


def one_axis_at_a_time(shard, axes):
    for axis in axes:
        shard = lax.psum(shard, axis)
    return shard


def probe_signs(row_keys, col_keys):
    hashed = jnp.bitwise_xor(row_keys[:, None] * 747796405, col_keys[None, :])
    hashed = jnp.bitwise_xor(hashed, jnp.right_shift(hashed, 15) & 131071)
    hashed = hashed * 695872825
    hashed = jnp.bitwise_xor(hashed, jnp.right_shift(hashed, 13) & 524287)
    hashed = hashed * 739982445
    hashed = jnp.bitwise_xor(hashed, jnp.right_shift(hashed, 16) & 65535)
    parity = jnp.right_shift(hashed, 11) & 1
    return (2 * parity - 1).astype(jnp.bfloat16)


def gelu_parts(preact):
    tanh_arg = gelu_coef * (preact + cubic_coef * preact * preact * preact)
    tanh_val = jnp.tanh(tanh_arg)
    sech_sq = 1.0 - tanh_val * tanh_val
    arg_slope = gelu_coef * (1.0 + 3.0 * cubic_coef * preact * preact)
    arg_curve = gelu_coef * 6.0 * cubic_coef * preact
    gelu_value = 0.5 * preact * (1.0 + tanh_val)
    gelu_slope = 0.5 * (1.0 + tanh_val) + 0.5 * preact * sech_sq * arg_slope
    gelu_curve = sech_sq * (
        arg_slope - preact * tanh_val * arg_slope * arg_slope + 0.5 * preact * arg_curve
    )
    return (gelu_value, gelu_slope, gelu_curve)


def body(tokens, targets, live_mask, up_weight, down_weight, probe_rows, probe_cols, moment):
    tok_count = tokens.shape[0]
    ff_local = up_weight.shape[1]
    own_rows = up_weight.shape[0]
    tensor_count = lax.axis_size("tensor")
    live_rows = live_mask.astype(jnp.float32)
    local_count = jnp.sum(live_rows) * (1.0 / tensor_count)
    all_signs = probe_signs(probe_rows, probe_cols)
    columns = tokens
    sign_rows = all_signs
    joined = jnp.concatenate([lax.all_gather(up_weight, DP, axis=0, tiled=True), sign_rows], axis=1)
    both_pre = jnp.dot(columns, joined, preferred_element_type=jnp.float32)
    preact = both_pre[:, :ff_local]
    tangent = both_pre[:, ff_local:]
    full_down = lax.all_gather(down_weight, DP, axis=0, tiled=True)
    gelu_value, gelu_slope, gelu_curve = gelu_parts(preact)
    hidden = gelu_value.astype(jnp.bfloat16)
    hidden_dir = (gelu_slope * tangent).astype(jnp.bfloat16)
    stacked = jnp.concatenate([hidden, hidden_dir], axis=0)
    projected = jnp.einsum("tf,df->td", stacked, full_down, preferred_element_type=jnp.float32)
    outputs, out_dir = together((projected[:tok_count], projected[tok_count:]), "tensor")
    diff = outputs - targets.astype(jnp.float32)
    weighted = live_rows[:, None] * diff
    local_loss = jnp.sum(weighted * diff) * (1.0 / tensor_count)
    residual = weighted.astype(jnp.bfloat16)
    residual_dir = (live_rows[:, None] * out_dir).astype(jnp.bfloat16)
    back_prod = jnp.dot(
        jnp.concatenate([residual, residual_dir], axis=0),
        full_down,
        preferred_element_type=jnp.float32,
    )
    grad_h = back_prod[:tok_count]
    grad_dir = back_prod[tok_count:]
    chain_grad = (grad_dir * gelu_slope + grad_h * gelu_curve * tangent).astype(jnp.bfloat16)
    columns = tokens
    product = jnp.einsum("tr,tf->rf", columns, chain_grad, preferred_element_type=jnp.float32)
    sign_rows = all_signs
    hutch_terms = sign_rows.astype(jnp.float32) * product
    own_share = sum_in_two_steps(
        hutch_terms.reshape(own_rows * lax.axis_size(DP), ff_local // BLOCK, BLOCK).mean(axis=-1),
        (("dp_0", "dp_1", "dp_2"), "dp_3"),
        0,
    )
    loss_sum, total_count = (
        one_axis_at_a_time(local_loss, DP_TENSOR),
        one_axis_at_a_time(local_count, DP_TENSOR),
    )
    hess_diag = own_share / total_count
    second_moment = beta_two * moment + (1.0 - beta_two) * hess_diag * hess_diag
    mean_loss = loss_sum / (2.0 * total_count)
    return (hess_diag, second_moment, mean_loss)


def solution(mesh):
    torus = Mesh(
        mesh.devices.reshape(4, 4, 4, 2, mesh.shape["tensor"]),
        ("dp_0", "dp_1", "dp_2", "dp_3", "tensor"),
    )
    placed = (
        P(DP, None),
        P(DP, None),
        P(DP),
        P(DP, "tensor"),
        P(DP, "tensor"),
        P(),
        P("tensor"),
        P(DP, "tensor"),
    )
    return jax.shard_map(
        body,
        mesh=torus,
        in_specs=placed,
        out_specs=(P(DP, "tensor"), P(DP, "tensor"), P()),
        check_vma=False,
    )
```

profile of v0, /device:TPU:1, one launch (start us, length us, event | category | flops | bytes accessed | tf_op | source)
XLA Modules:
  0.0 491.9 jit_solution(3638978809061497128)
XLA Ops:
  9.4 15.8 %add_convert_fusion = bf16[1792,3584]{0,1:T(8,128)(2,1)} fusion(s32[3584]{0:T(1024)} %param.14, s32[1792]{0:T(1024)S(1)} %broadcast_multiply_fusion.1), kind=kLoop, calls=%fused_computation.13 | loop fusion | flops 109182976 | bytes 12866560 | tf_op jit(solution)/shard_map/convert_element_type | solution.py:65
  25.2 99.8 %all-gather.5.cloned.1.call-done = bf16[128,14,3584]{2,1,0:T(8,128)(2,1)} async-done(((bf16[1,14,3584]{2,1,0:T(8,128)(2,1)}), bf16[128,14,3584]{2,1,0:T(8,128)(2,1)}) %all-gather.5.cloned.1.call-update) | async-done | bytes 12845072 | tf_op jit(solution)/shard_map/all_gather | solution.py:92
  125.0 16.8 %reshape.48 = bf16[1792,3584]{1,0:T(8,128)(2,1)} reshape(bf16[128,14,3584]{2,1,0:T(8,128)(2,1)} %all-gather.5.cloned.1.call-done) | data formatting | bytes 25690112
  141.9 17.9 %copy.27 = bf16[1792,3584]{0,1:T(8,128)(2,1)} copy(bf16[1792,3584]{1,0:T(8,128)(2,1)} %reshape.48) | data formatting | bytes 25690112
  159.8 15.2 %fusion.10 = f32[128,7168]{1,0:T(8,128)} fusion(bf16[128,1792]{1,0:T(8,128)(2,1)S(1)} %copy-done, bf16[1792,3584]{0,1:T(8,128)(2,1)} %add_convert_fusion, bf16[1792,3584]{0,1:T(8,128)(2,1)} %copy.27), kind=kOutput, calls=%fused_computation.14 | convolution fusion | flops 3339714560 | bytes 29818880 | tf_op jit(solution)/shard_map/dot_general | solution.py:93
  175.0 3.3 multiply_convert_fusion.1
  178.3 57.5 %all-gather.7.cloned.1.call-done = bf16[128,14,3584]{2,1,0:T(8,128)(2,1)} async-done(((bf16[1,14,3584]{2,1,0:T(8,128)(2,1)}), bf16[128,14,3584]{2,1,0:T(8,128)(2,1)}) %all-gather.7.cloned.1.call-update) | async-done | bytes 12845072 | tf_op jit(solution)/shard_map/all_gather | solution.py:96
  235.8 16.8 %reshape.50 = bf16[1792,3584]{1,0:T(8,128)(2,1)} reshape(bf16[128,14,3584]{2,1,0:T(8,128)(2,1)} %all-gather.7.cloned.1.call-done) | data formatting | bytes 25690112
  252.6 7.0 %fusion.23 = f32[256,1792]{1,0:T(8,128)S(1)} fusion(bf16[1792,3584]{1,0:T(8,128)(2,1)} %reshape.50, bf16[128,3584]{1,0:T(8,128)(2,1)S(1)} %get-tuple-element.16, bf16[128,3584]{1,0:T(8,128)(2,1)S(1)} %get-tuple-element.15), kind=kOutput, calls=%fused_computation.29 | convolution fusion | flops 3292004352 | bytes 16515072 | tf_op jit(solution)/shard_map/tf,df->td/dot_general | solution.py:101
  260.1 3.3 broadcast_in_dim.2
  263.3 5.7 %all-to-all-start = ((f32[2,1,458752]{2,1,0:T(1,128)}), f32[2,1,458752]{2,1,0:T(1,128)}, u32[]{:S(2)}, u32[]{:S(2)}) async-start(f32[2,1,458752]{2,1,0:T(1,128)} %broadcast_in_dim.2), calls=%async_computation | async-start | bytes 7340032 | tf_op jit(solution)/shard_map/all_to_all | solution.py:17
  269.1 41.4 %all-to-all-done = f32[2,1,458752]{2,1,0:T(1,128)} async-done(((f32[2,1,458752]{2,1,0:T(1,128)}), f32[2,1,458752]{2,1,0:T(1,128)}, u32[]{:S(2)}, u32[]{:S(2)}) %all-to-all-start) | async-done | bytes 3670048 | tf_op jit(solution)/shard_map/all_to_all | solution.py:17
  310.5 18.1 %reduce_sum.54 = f32[458752]{0:T(1024)S(1)} reduce(f32[2,1,458752]{2,1,0:T(1,128)} %all-to-all-done, f32[]{:T(128)} %constant.20.clone.1), dimensions={0,1}, to_apply=%region_0.0 | reduce | flops 458752 | bytes 5505028 | tf_op jit(solution)/shard_map/reduce_sum | solution.py:22
  329.7 1.3 slice.49
  331.2 2.0 fusion.27
  333.1 6.7 %fusion.29 = f32[256,3584]{1,0:T(8,128)S(1)} fusion(bf16[1792,3584]{1,0:T(8,128)(2,1)} %reshape.50, bf16[128,1792]{1,0:T(8,128)(2,1)S(1)} %get-tuple-element.23, bf16[128,1792]{1,0:T(8,128)(2,1)S(1)} %get-tuple-element.22), kind=kOutput, calls=%fused_computation.41 | convolution fusion | flops 3290169344 | bytes 17432576 | tf_op jit(solution)/shard_map/dot_general | solution.py:108
  339.8 17.9 %bitcast_multiply_fusion = f32[1792,3584]{0,1:T(8,128)} fusion(bf16[128,1792]{1,0:T(8,128)(2,1)S(1)} %copy-done, s32[3584]{0:T(1024)S(1)} %copy-done.3, s32[1792]{0:T(1024)S(1)} %broadcast_multiply_fusion.1, f32[256,3584]{1,0:T(8,128)S(1)} %fusion.29, f32[128,7168]{1,0:T(8,128)S(1)} %copy-done.2), kind=kOutput, calls=%fused_computation.12 | convolution fusion | flops 1779957760 | bytes 33510400 | tf_op jit(solution)/shard_map/tr,tf->rf/dot_general | solution.py:117
  357.7 26.7 %reshape.46 = f32[1792,256,14]{0,2,1:T(8,128)} reshape(f32[1792,3584]{0,1:T(8,128)} %bitcast_multiply_fusion) | data formatting | bytes 51380224 | tf_op jit(solution)/shard_map/reshape | solution.py:121
  384.4 13.6 %reduce_sum.55 = f32[1792,256]{0,1:T(8,128)} reduce(f32[1792,256,14]{0,2,1:T(8,128)} %reshape.46, f32[]{:T(128)} %constant.20.clone.1), dimensions={2}, to_apply=%region_1.0 | reduce | flops 5963776 | bytes 27525124 | tf_op jit(solution)/shard_map/reduce_sum | solution.py:121
  398.0 1.7 broadcast_multiply_fusion
  399.7 1.7 copy.29
  401.4 1.6 div.19
  403.0 1.1 copy.30
  404.1 6.1 %all_to_all.16 = f32[2,64,14,256]{3,1,2,0:T(8,128)S(1)} all-to-all(f32[2,64,14,256]{3,1,2,0:T(8,128)S(1)} %copy.30), channel_id=1, replica_groups=mesh['dp_0'=4,'dp_1'=4,'dp_2'=4,'dp_3'=2,'tensor'=2] {'dp_3'}, dimensions={0} | all-to-all | bytes 3670016 | tf_op jit(solution)/shard_map/all_to_all | solution.py:41
  410.4 1.5 copy.31
  411.9 9.3 %all-to-all-start.2 = ((f32[64,14,256]{2,1,0:T(8,128)}), f32[64,14,256]{2,1,0:T(8,128)S(1)}, u32[]{:S(2)}, u32[]{:S(2)}) async-start(f32[64,14,256]{2,1,0:T(8,128)} %copy.31), calls=%async_computation.2 | async-start | bytes 2097152 | tf_op jit(solution)/shard_map/all_to_all | solution.py:48
  423.1 26.9 %all-reduce.2 = (f32[]{:T(128)}, f32[]{:T(128)}) all-reduce(f32[]{:T(128)S(6)} %mul.184, f32[]{:T(128)S(6)} %mul.191), channel_id=1, replica_groups=mesh['dp_0'=4,'dp_1'=4,'dp_2'=4,'dp_3'=2,'tensor'=2] {'dp_0'}, use_global_device_ids=true, to_apply=%region_5.0 | all-reduce | flops 2 | bytes 16 | tf_op jit(solution)/shard_map/psum | solution.py:53
  450.1 8.9 %all-reduce.1 = (f32[]{:T(128)}, f32[]{:T(128)}) all-reduce(f32[]{:T(128)} %get-tuple-element.7, f32[]{:T(128)} %get-tuple-element.8), channel_id=1, replica_groups=mesh['dp_0'=4,'dp_1'=4,'dp_2'=4,'dp_3'=2,'tensor'=2] {'dp_1'}, use_global_device_ids=true, to_apply=%region_6.0 | all-reduce | flops 2 | bytes 16 | tf_op jit(solution)/shard_map/psum | solution.py:53
  459.0 8.8 %all-reduce = (f32[]{:T(128)}, f32[]{:T(128)}) all-reduce(f32[]{:T(128)} %get-tuple-element.5, f32[]{:T(128)} %get-tuple-element.6), channel_id=1, replica_groups=mesh['dp_0'=4,'dp_1'=4,'dp_2'=4,'dp_3'=2,'tensor'=2] {'dp_2'}, use_global_device_ids=true, to_apply=%region_7.0 | all-reduce | flops 2 | bytes 16 | tf_op jit(solution)/shard_map/psum | solution.py:53
  467.8 8.8 %all-reduce.4 = (f32[]{:T(128)}, f32[]{:T(128)}) all-reduce(f32[]{:T(128)} %get-tuple-element.3, f32[]{:T(128)} %get-tuple-element.4), channel_id=1, replica_groups=mesh['dp_0'=4,'dp_1'=4,'dp_2'=4,'dp_3'=2,'tensor'=2] {'dp_3'}, use_global_device_ids=true, to_apply=%region_8.0 | all-reduce | flops 2 | bytes 16 | tf_op jit(solution)/shard_map/psum | solution.py:53
  476.5 4.6 all-reduce.3
  482.7 1.3 fusion.39
  (28 shorter events, 4.7 us)
Async XLA Ops:
  7.2 152.6 %copy-start = (bf16[128,1792]{1,0:T(8,128)(2,1)S(1)}, bf16[128,1792]{1,0:T(8,128)(2,1)}, u32[]{:S(2)}) copy-start(bf16[128,1792]{1,0:T(8,128)(2,1)} %param.8) | copy-start | bytes 1376260
  7.2 117.9 %all-gather.5.cloned.1.call-start = ((), (), s32[]{:S(2)}) async-start(), calls=%async_computation.3 | async-start | bytes 14794752 | tf_op jit(solution)/shard_map/all_gather | solution.py:92
  7.9 227.9 %all-gather.7.cloned.1.call-start = ((), (), s32[]{:S(2)}) async-start(), calls=%async_computation.4 | async-start | bytes 14794752 | tf_op jit(solution)/shard_map/all_gather | solution.py:96
  263.3 5.7 %copy-start.5 = (s32[128]{0:T(128)S(1)}, s32[128]{0:T(128)}, u32[]{:S(2)}) copy-start(s32[128]{0:T(128)} %param.10) | copy-start | bytes 1540
  263.3 47.2 %all-to-all-start = ((f32[2,1,458752]{2,1,0:T(1,128)}), f32[2,1,458752]{2,1,0:T(1,128)}, u32[]{:S(2)}, u32[]{:S(2)}) async-start(f32[2,1,458752]{2,1,0:T(1,128)} %broadcast_in_dim.2), calls=%async_computation | async-start | bytes 7340032 | tf_op jit(solution)/shard_map/all_to_all | solution.py:17
  333.1 6.7 %copy-start.2 = (f32[128,7168]{1,0:T(8,128)S(1)}, f32[128,7168]{1,0:T(8,128)}, u32[]{:S(2)}) copy-start(f32[128,7168]{1,0:T(8,128)} %fusion.10) | copy-start | bytes 11010052
  333.1 6.7 %copy-start.3 = (s32[3584]{0:T(1024)S(1)}, s32[3584]{0:T(1024)}, u32[]{:S(2)}) copy-start(s32[3584]{0:T(1024)} %param.14) | copy-start | bytes 43012
  404.1 79.9 %copy-start.1 = (bf16[128,1792]{1,0:T(8,128)(2,1)S(1)}, bf16[128,1792]{1,0:T(8,128)(2,1)}, u32[]{:S(2)}) copy-start(bf16[128,1792]{1,0:T(8,128)(2,1)} %param.8) | copy-start | bytes 1376260
  410.2 72.5 %copy-start.4 = (f32[14,256]{1,0:T(8,128)S(1)}, f32[14,256]{1,0:T(8,128)}, u32[]{:S(2)}) copy-start(f32[14,256]{1,0:T(8,128)} %param.15) | copy-start | bytes 43012
  411.9 70.6 %all-to-all-start.2 = ((f32[64,14,256]{2,1,0:T(8,128)}), f32[64,14,256]{2,1,0:T(8,128)S(1)}, u32[]{:S(2)}, u32[]{:S(2)}) async-start(f32[64,14,256]{2,1,0:T(8,128)} %copy.31), calls=%async_computation.2 | async-start | bytes 2097152 | tf_op jit(solution)/shard_map/all_to_all | solution.py:48
Sparse Core Ops, SparseCore 0:
  11.4 113.6 all-gather.4
  128.5 107.3 all-gather.6
where the time goes:
time: 495 us; the launch traced here: 492 us
  waiting for transfers between devices  200 us (40%)
  local copies, waits for them, and re-layouts  90.2 us (18%)
  blocking collectives  64.2 us (13%)
  other arithmetic  57.6 us (12%)
  matrix products  46.8 us (9%)
  between operations  18 us (4%)
  starting transfers between devices  15.1 us (3%)
    all_gather x1, waiting for transfers between devices, body(): lax.all_gather(up_weight, DP, axis=0, tiled=True)  99.8 us
    psum x5, blocking collectives, one_axis_at_a_time(): shard = lax.psum(shard, axis)  58.1 us
    all_gather x1, waiting for transfers between devices, body(): full_down = lax.all_gather(down_weight, DP, axis=0, tiled=True)  57.5 us
    unnamed x15, local copies, waits for them, and re-layouts  51.6 us
    all_to_all x1, waiting for transfers between devices, sent_to_all(): return lax.all_to_all(copies, axis, split_axis=0, concat_axis=0, tiled=True)  41.4 us
    reshape x1, local copies, waits for them, and re-layouts, body(): hutch_terms.reshape(own_rows * lax.axis_size(DP), ff_local // BLOCK, BLOCK)  26.7 us
    reduce_sum x1, other arithmetic, over_copies(): return jnp.sum(everything, axis=0)  18.1 us
    dot_general x1, matrix products, body(): jnp.einsum('tr,tf->rf', columns, chain_grad, preferred_element_type=jnp.f...  17.9 us
  transfers between devices with their start and end apart: 4, of which 3 were waited for; matrix products, arithmetic and copies ran while one was open for 14% of the time, Pallas kernels for 0%

commit v1 on v0

--- a/solution.py
+++ b/solution.py
@@ -93,7 +93,9 @@
     both_pre = jnp.dot(columns, joined, preferred_element_type=jnp.float32)
     preact = both_pre[:, :ff_local]
     tangent = both_pre[:, ff_local:]
-    full_down = lax.all_gather(down_weight, DP, axis=0, tiled=True)
+    full_down = jnp.concatenate(
+        lax.all_to_all(jnp.stack([down_weight] * lax.axis_size(DP)), DP, 0, 0), axis=0
+    )
     gelu_value, gelu_slope, gelu_curve = gelu_parts(preact)
     hidden = gelu_value.astype(jnp.bfloat16)
     hidden_dir = (gelu_slope * tangent).astype(jnp.bfloat16)

time: 495 us -> 714 us (1.44)
  waiting for transfers between devices: 200 us -> 351 us
  starting transfers between devices: 15.1 us -> 76.5 us
  local copies, waits for them, and re-layouts: 90.2 us -> 98.1 us
    all_gather x1, waiting for transfers between devices: 99.8 us -> 251 us  [body(): lax.all_gather(up_weight, DP, axis=0, tiled=True)]
    all_to_all x0 -> x1, waiting for transfers between devices: none -> 58.3 us  [body(): lax.all_to_all(jnp.stack([down_weight] * lax.axis_size(DP)), DP, 0, 0)]
    all_gather x1 -> x0, waiting for transfers between devices: 57.5 us -> none  [body(): full_down = lax.all_gather(down_weight, DP, axis=0, tiled=True)]
    all_to_all x1, starting transfers between devices: 9.28 us -> 53.8 us  [sum_in_two_steps(): return jnp.sum(lax.all_to_all(own, far, 0, 0, tiled=True), axis=0)]
    all_to_all x0 -> x1, starting transfers between devices: none -> 16.9 us  [body(): lax.all_to_all(jnp.stack([down_weight] * lax.axis_size(DP)), DP, 0, 0)]
    unnamed x15 -> x16, local copies, waits for them, and re-layouts: 51.6 us -> 34.8 us
    reshape x0 -> x1, local copies, waits for them, and re-layouts: none -> 16.8 us  [body(): jnp.concatenate(lax.all_to_all(jnp.stack([down_weight] * lax.axis_size(DP...]
    another operation x0 -> x1, local copies, waits for them, and re-layouts: none -> 7.92 us  [body(): jnp.stack([down_weight] * lax.axis_size(DP))]
  transfers between devices with their start and end apart: 4 -> 4, of which waited for: 3 -> 3; matrix products, arithmetic and copies ran while one was open for 14% -> 11% of each run, Pallas kernels for 0% -> 0%
where the time goes in v1:
time: 714 us; the launch traced here: 712 us
  waiting for transfers between devices  351 us (49%)
  local copies, waits for them, and re-layouts  98.1 us (14%)
  starting transfers between devices  76.5 us (11%)
  blocking collectives  64.7 us (9%)
  other arithmetic  56.5 us (8%)
  matrix products  46.5 us (7%)
  between operations  18 us (3%)
    all_gather x1, waiting for transfers between devices, body(): lax.all_gather(up_weight, DP, axis=0, tiled=True)  251 us
    all_to_all x1, waiting for transfers between devices, body(): lax.all_to_all(jnp.stack([down_weight] * lax.axis_size(DP)), DP, 0, 0)  58.3 us
    psum x5, blocking collectives, one_axis_at_a_time(): shard = lax.psum(shard, axis)  58.1 us
    all_to_all x1, starting transfers between devices, sum_in_two_steps(): return jnp.sum(lax.all_to_all(own, far, 0, 0, tiled=True), axis=0)  53.8 us
    all_to_all x1, waiting for transfers between devices, sent_to_all(): return lax.all_to_all(copies, axis, split_axis=0, concat_axis=0, tiled=True)  40.8 us
    unnamed x16, local copies, waits for them, and re-layouts  34.8 us
    reshape x1, local copies, waits for them, and re-layouts, body(): hutch_terms.reshape(own_rows * lax.axis_size(DP), ff_local // BLOCK, BLOCK)  26.7 us
    reduce_sum x1, other arithmetic, over_copies(): return jnp.sum(everything, axis=0)  18.1 us
  transfers between devices with their start and end apart: 4, of which 3 were waited for; matrix products, arithmetic and copies ran while one was open for 11% of the time, Pallas kernels for 0%

profile of v1, /device:TPU:1, one launch (start us, length us, event | category | flops | bytes accessed | tf_op | source)
XLA Modules:
  0.0 711.7 jit_solution(13795887788868413789)
XLA Ops:
  7.9 7.9 %stack.2 = bf16[128,14,3584]{2,1,0:T(8,128)(2,1)} broadcast(bf16[14,3584]{1,0:T(8,128)(2,1)} %param.12), dimensions={1,2} | broadcast | bytes 12945408 | tf_op jit(solution)/shard_map/stack | solution.py:97
  15.8 16.9 %all-to-all-start = ((bf16[128,14,3584]{2,1,0:T(8,128)(2,1)}), bf16[128,14,3584]{2,1,0:T(8,128)(2,1)}, u32[]{:S(2)}, u32[]{:S(2)}) async-start(bf16[128,14,3584]{2,1,0:T(8,128)(2,1)} %stack.2), calls=%async_computation | async-start | bytes 29360128 | tf_op jit(solution)/shard_map/all_to_all | solution.py:97
  32.8 15.5 %add_convert_fusion = bf16[1792,3584]{0,1:T(8,128)(2,1)} fusion(s32[3584]{0:T(1024)S(1)} %copy-done.3, s32[1792]{0:T(1024)S(1)} %broadcast_multiply_fusion.1), kind=kLoop, calls=%fused_computation.13 | loop fusion | flops 109182976 | bytes 12866560 | tf_op jit(solution)/shard_map/convert_element_type | solution.py:65
  48.3 251.4 %all-gather.3.cloned.1.call-done = bf16[128,14,3584]{2,1,0:T(8,128)(2,1)} async-done(((bf16[1,14,3584]{2,1,0:T(8,128)(2,1)}), bf16[128,14,3584]{2,1,0:T(8,128)(2,1)}) %all-gather.3.cloned.1.call-update) | async-done | bytes 12845072 | tf_op jit(solution)/shard_map/all_gather | solution.py:92
  299.8 16.8 %reshape.54 = bf16[1792,3584]{1,0:T(8,128)(2,1)} reshape(bf16[128,14,3584]{2,1,0:T(8,128)(2,1)} %all-gather.3.cloned.1.call-done) | data formatting | bytes 25690112
  316.6 17.9 %copy.27 = bf16[1792,3584]{0,1:T(8,128)(2,1)} copy(bf16[1792,3584]{1,0:T(8,128)(2,1)} %reshape.54) | data formatting | bytes 25690112
  334.5 15.0 %fusion.10 = f32[128,7168]{1,0:T(8,128)} fusion(bf16[128,1792]{1,0:T(8,128)(2,1)S(1)} %copy-done, bf16[1792,3584]{0,1:T(8,128)(2,1)} %add_convert_fusion, bf16[1792,3584]{0,1:T(8,128)(2,1)} %copy.27), kind=kOutput, calls=%fused_computation.14 | convolution fusion | flops 3339714560 | bytes 29818880 | tf_op jit(solution)/shard_map/dot_general | solution.py:93
  349.5 3.3 multiply_convert_fusion.1
  352.8 58.3 %all-to-all-done = bf16[128,14,3584]{2,1,0:T(8,128)(2,1)} async-done(((bf16[128,14,3584]{2,1,0:T(8,128)(2,1)}), bf16[128,14,3584]{2,1,0:T(8,128)(2,1)}, u32[]{:S(2)}, u32[]{:S(2)}) %all-to-all-start) | async-done | bytes 12845088 | tf_op jit(solution)/shard_map/all_to_all | solution.py:97
  411.0 16.8 %reshape.49 = bf16[1792,3584]{1,0:T(8,128)(2,1)} reshape(bf16[128,14,3584]{2,1,0:T(8,128)(2,1)} %all-to-all-done) | data formatting | bytes 25690112 | tf_op jit(solution)/shard_map/reshape | solution.py:96
  427.8 7.0 fusion.23
  435.2 3.3 broadcast_in_dim.2
  438.5 5.7 all-to-all-start.1
  444.3 40.8 %all-to-all-done.1 = f32[2,1,458752]{2,1,0:T(1,128)} async-done(((f32[2,1,458752]{2,1,0:T(1,128)}), f32[2,1,458752]{2,1,0:T(1,128)}, u32[]{:S(2)}, u32[]{:S(2)}) %all-to-all-start.1) | async-done | bytes 3670048 | tf_op jit(solution)/shard_map/all_to_all | solution.py:17
  485.1 18.1 %reduce_sum.54 = f32[458752]{0:T(1024)S(1)} reduce(f32[2,1,458752]{2,1,0:T(1,128)} %all-to-all-done.1, f32[]{:T(128)} %constant.20.clone.1), dimensions={0,1}, to_apply=%region_0.0 | reduce | flops 458752 | bytes 5505028 | tf_op jit(solution)/shard_map/reduce_sum | solution.py:22
  504.3 1.3 slice.49
  505.8 2.0 fusion.27
  507.7 6.7 fusion.29
  514.4 17.9 %bitcast_multiply_fusion = f32[1792,3584]{0,1:T(8,128)} fusion(bf16[128,1792]{1,0:T(8,128)(2,1)S(1)} %copy-done, s32[3584]{0:T(1024)S(1)} %copy-done.3, s32[1792]{0:T(1024)S(1)} %broadcast_multiply_fusion.1, f32[256,3584]{1,0:T(8,128)S(1)} %fusion.29, f32[128,7168]{1,0:T(8,128)S(1)} %copy-done.2), kind=kOutput, calls=%fused_computation.12 | convolution fusion | flops 1779957760 | bytes 33510400 | tf_op jit(solution)/shard_map/tr,tf->rf/dot_general | solution.py:119
  532.3 26.7 %reshape.52 = f32[1792,256,14]{0,2,1:T(8,128)} reshape(f32[1792,3584]{0,1:T(8,128)} %bitcast_multiply_fusion) | data formatting | bytes 51380224 | tf_op jit(solution)/shard_map/reshape | solution.py:123
  559.0 13.6 %reduce_sum.55 = f32[1792,256]{0,1:T(8,128)} reduce(f32[1792,256,14]{0,2,1:T(8,128)} %reshape.52, f32[]{:T(128)} %constant.20.clone.1), dimensions={2}, to_apply=%region_1.0 | reduce | flops 5963776 | bytes 27525124 | tf_op jit(solution)/shard_map/reduce_sum | solution.py:123
  572.7 1.7 broadcast_multiply_fusion
  574.3 1.7 copy.29
  576.1 1.6 div.19
  578.7 6.6 all_to_all.21
  585.6 1.5 copy.31
  587.1 53.8 %all-to-all-start.3 = ((f32[64,14,256]{2,1,0:T(8,128)}), f32[64,14,256]{2,1,0:T(8,128)S(1)}, u32[]{:S(2)}, u32[]{:S(2)}) async-start(f32[64,14,256]{2,1,0:T(8,128)} %copy.31), calls=%async_computation.3 | async-start | bytes 2097152 | tf_op jit(solution)/shard_map/all_to_all | solution.py:48
  642.8 26.9 %all-reduce.2 = (f32[]{:T(128)}, f32[]{:T(128)}) all-reduce(f32[]{:T(128)S(6)} %mul.184, f32[]{:T(128)S(6)} %mul.191), channel_id=1, replica_groups=mesh['dp_0'=4,'dp_1'=4,'dp_2'=4,'dp_3'=2,'tensor'=2] {'dp_0'}, use_global_device_ids=true, to_apply=%region_5.0 | all-reduce | flops 2 | bytes 16 | tf_op jit(solution)/shard_map/psum | solution.py:53
  669.8 8.9 %all-reduce.1 = (f32[]{:T(128)}, f32[]{:T(128)}) all-reduce(f32[]{:T(128)} %get-tuple-element.7, f32[]{:T(128)} %get-tuple-element.8), channel_id=1, replica_groups=mesh['dp_0'=4,'dp_1'=4,'dp_2'=4,'dp_3'=2,'tensor'=2] {'dp_1'}, use_global_device_ids=true, to_apply=%region_6.0 | all-reduce | flops 2 | bytes 16 | tf_op jit(solution)/shard_map/psum | solution.py:53
  678.7 8.8 %all-reduce = (f32[]{:T(128)}, f32[]{:T(128)}) all-reduce(f32[]{:T(128)} %get-tuple-element.5, f32[]{:T(128)} %get-tuple-element.6), channel_id=1, replica_groups=mesh['dp_0'=4,'dp_1'=4,'dp_2'=4,'dp_3'=2,'tensor'=2] {'dp_2'}, use_global_device_ids=true, to_apply=%region_7.0 | all-reduce | flops 2 | bytes 16 | tf_op jit(solution)/shard_map/psum | solution.py:53
  687.5 8.8 %all-reduce.4 = (f32[]{:T(128)}, f32[]{:T(128)}) all-reduce(f32[]{:T(128)} %get-tuple-element.3, f32[]{:T(128)} %get-tuple-element.4), channel_id=1, replica_groups=mesh['dp_0'=4,'dp_1'=4,'dp_2'=4,'dp_3'=2,'tensor'=2] {'dp_3'}, use_global_device_ids=true, to_apply=%region_8.0 | all-reduce | flops 2 | bytes 16 | tf_op jit(solution)/shard_map/psum | solution.py:53
  696.3 4.6 all-reduce.3
  (30 shorter events, 5.6 us)
Async XLA Ops:
  7.2 327.3 %copy-start = (bf16[128,1792]{1,0:T(8,128)(2,1)S(1)}, bf16[128,1792]{1,0:T(8,128)(2,1)}, u32[]{:S(2)}) copy-start(bf16[128,1792]{1,0:T(8,128)(2,1)} %param.8) | copy-start | bytes 1376260
  7.2 292.6 %all-gather.3.cloned.1.call-start = ((), (), s32[]{:S(2)}) async-start(), calls=%async_computation.4 | async-start | bytes 14794752 | tf_op jit(solution)/shard_map/all_gather | solution.py:92
  15.8 16.9 %copy-start.5 = (s32[1792]{0:T(1024)S(1)}, s32[1792]{0:T(1024)}, u32[]{:S(2)}) copy-start(s32[1792]{0:T(1024)} %param.13) | copy-start | bytes 21508
  15.8 17.0 %copy-start.3 = (s32[3584]{0:T(1024)S(1)}, s32[3584]{0:T(1024)}, u32[]{:S(2)}) copy-start(s32[3584]{0:T(1024)} %param.14) | copy-start | bytes 43012
  15.8 395.2 %all-to-all-start = ((bf16[128,14,3584]{2,1,0:T(8,128)(2,1)}), bf16[128,14,3584]{2,1,0:T(8,128)(2,1)}, u32[]{:S(2)}, u32[]{:S(2)}) async-start(bf16[128,14,3584]{2,1,0:T(8,128)(2,1)} %stack.2), calls=%async_computation | async-start | bytes 29360128 | tf_op jit(solution)/shard_map/all_to_all | solution.py:97
  438.5 5.7 copy-start.6
  438.5 46.6 %all-to-all-start.1 = ((f32[2,1,458752]{2,1,0:T(1,128)}), f32[2,1,458752]{2,1,0:T(1,128)}, u32[]{:S(2)}, u32[]{:S(2)}) async-start(f32[2,1,458752]{2,1,0:T(1,128)} %broadcast_in_dim.2), calls=%async_computation.1 | async-start | bytes 7340032 | tf_op jit(solution)/shard_map/all_to_all | solution.py:17
  507.7 6.7 copy-start.2
  578.7 125.0 %copy-start.1 = (bf16[128,1792]{1,0:T(8,128)(2,1)S(1)}, bf16[128,1792]{1,0:T(8,128)(2,1)}, u32[]{:S(2)}) copy-start(bf16[128,1792]{1,0:T(8,128)(2,1)} %param.8) | copy-start | bytes 1376260
  585.4 117.0 %copy-start.4 = (f32[14,256]{1,0:T(8,128)S(1)}, f32[14,256]{1,0:T(8,128)}, u32[]{:S(2)}) copy-start(f32[14,256]{1,0:T(8,128)} %param.15) | copy-start | bytes 43012
  587.1 115.2 %all-to-all-start.3 = ((f32[64,14,256]{2,1,0:T(8,128)}), f32[64,14,256]{2,1,0:T(8,128)S(1)}, u32[]{:S(2)}, u32[]{:S(2)}) async-start(f32[64,14,256]{2,1,0:T(8,128)} %copy.31), calls=%async_computation.3 | async-start | bytes 2097152 | tf_op jit(solution)/shard_map/all_to_all | solution.py:48
Sparse Core Ops, SparseCore 0:
  11.4 288.3 all-gather.2
